TPU v7x, 128 devices: a whole 4x4x4 slice. The times are simulated.
128 devices in a mesh: row: 8 (over z, y_hi), col: 16 (over y_lo, x, core).
Axes of the slice: x: 4, y: 4 (y_hi: 2, y_lo: 2; y = y_hi * 2 + y_lo), z: 4, core: 2. Of those that a mesh axis runs over, the one named last changes fastest.
Arguments:
- matrix_tiles: float32 [8, 16, 16, 512, 512], P('row', 'col'), may hold values from -0.25 to 0.25
- tile_rows: int32 [8, 16, 16], P('row', 'col'), may hold values from 0 to 127, as said below
- tile_columns: int32 [8, 16, 16], P('row', 'col'), may hold values from 0 to 63, as said below
- tile_counts: int32 [8, 16], P('row', 'col'), may hold values from 8 to 16, as said below
- primal_iter: float32 [2, 524288], P(None, ('col', 'row')), may hold values from -6 to 6
- dual_iter: float32 [2, 524288], P(None, ('row', 'col')), may hold values from -6 to 6
- requirement: float32 [524288], P('row'), may hold values from -68 to 68
- constraint_kind: int32 [524288], P('row'), may hold values from 0 to 1
- objective: float32 [524288], P('col'), may hold values from -68 to 68
- lower_bound: float32 [524288], P('col'), may hold values from -1.5 to 1.5
- upper_bound: float32 [524288], P('col'), may hold values from -1.5 to 1.5
- variable_kind: int32 [524288], P('col'), may hold values from 0 to 3
Outputs:
- primal_residual: float32 [2, 524288], P(None, ('row', 'col'))
- dual_residual: float32 [2, 524288], P(None, ('col', 'row'))
- metrics: float32 [2, 3], replicated
Inputs may be any that keep to these rules, and one draw needn't show every extreme that they name: `tile_counts`: slots below the count of a list hold live tiles, the others are padding; some list has all 16 slots live. `tile_rows`: in each constraint group, the first (8) slots of its lists name every block row of the group exactly once; later slots name any block row, and repeated tiles add. `tile_columns`: in each variable group, the first (8) slots of its lists name every block column of the group exactly once; later slots name any block column, and repeated tiles add. `constraint_kind`: 0 marks an equality, 1 a constraint of the form at least. `variable_kind`: 0 free, 1 lower bound only, 2 upper bound only, 3 both bounds.
All inputs are finite; a program needn't handle non-finite values.
Results may differ from a plain program's by a relative error of at most 0.0003.
Values sent between devices are 32-bit elements; how exact they have to be, the bound alone decides.
A program may use at most 64 MiB of HBM per device.

v0:
```python
import jax
import jax.numpy as jnp
from jax import lax
from jax.sharding import Mesh
from jax.sharding import PartitionSpec as P

ROW = ("row_0", "row_1")
COL = ("col_0", "col_1", "col_2")
ROW_COL = ("row_0", "row_1", "col_0", "col_1", "col_2")
COL_ROW = ("col_0", "col_1", "col_2", "row_0", "row_1")
HIGHEST_PRECISION = lax.Precision.HIGHEST


def from_everyone(shard, axis):
    copies = jnp.broadcast_to(shard, (lax.axis_size(axis), *shard.shape))
    return lax.all_to_all(copies, axis, split_axis=0, concat_axis=0, tiled=True)


def joined_along(pieces, dim):
    lengths = list(pieces.shape[1:])
    lengths[dim] *= pieces.shape[0]
    return jnp.moveaxis(pieces, 0, dim).reshape(lengths)


def collect(shard, axis, dim):
    pieces = from_everyone(shard, axis)
    return joined_along(pieces, dim)


def cut_along(shard, dim, count):
    lengths = shard.shape
    pieces = shard.reshape(*lengths[:dim], count, lengths[dim] // count, *lengths[dim + 1 :])
    return jnp.moveaxis(pieces, dim, 0)


def sum_at_owner(shard, axis, dim):
    count = lax.axis_size(axis)
    pieces = lax.all_to_all(cut_along(shard, dim, count), axis, 0, 0, tiled=True)
    return jnp.sum(pieces, axis=0)


def one_axis_at_a_time(shard, axes):
    for axis in axes:
        shard = lax.psum(shard, axis)
    return shard


def primal_side(product, require_part, kind_part, dual_part):
    difference = require_part[None, :] - product
    residual = jnp.where(kind_part[None, :] == 1, jnp.maximum(difference, 0.0), difference)
    return (
        residual,
        jnp.sum(residual * residual, axis=1),
        jnp.sum(require_part * require_part),
        jnp.sum(require_part[None, :] * dual_part, axis=1),
    )


def dual_side(transposed, objective, lower_bound, upper_bound, variable_kind, primal_part):
    reduced = objective[None, :] - transposed
    lower_active = (variable_kind == 1) | (variable_kind == 3)
    upper_active = (variable_kind == 2) | (variable_kind == 3)
    multiplier = jnp.where(lower_active[None, :], jnp.maximum(reduced, 0.0), 0.0) + jnp.where(
        upper_active[None, :], jnp.minimum(reduced, 0.0), 0.0
    )
    residual = reduced - multiplier
    bound_sum = jnp.sum(
        lower_bound[None, :] * jnp.maximum(multiplier, 0.0)
        + upper_bound[None, :] * jnp.minimum(multiplier, 0.0),
        axis=1,
    )
    return (
        residual,
        jnp.sum(residual * residual, axis=1),
        jnp.sum(objective * objective),
        jnp.sum(objective[None, :] * primal_part, axis=1),
        bound_sum,
    )


def finish(
    primal_square,
    require_square,
    require_dot,
    dual_square,
    objective_square,
    objective_dot,
    bound_sum,
):
    primal_ratio = jnp.sqrt(primal_square) / (1.0 + jnp.sqrt(require_square))
    dual_ratio = jnp.sqrt(dual_square) / (1.0 + jnp.sqrt(objective_square))
    dual_value = require_dot + bound_sum
    duality_gap = jnp.abs(objective_dot - dual_value) / (
        1.0 + jnp.abs(objective_dot) + jnp.abs(dual_value)
    )
    return jnp.stack([primal_ratio, dual_ratio, duality_gap], axis=1)


def on_device(
    matrix_tiles,
    tile_rows,
    tile_columns,
    tile_counts,
    primal_iter,
    dual_iter,
    requirement,
    constraint_kind,
    objective,
    lower_bound,
    upper_bound,
    variable_kind,
):
    own_tiles = matrix_tiles[0, 0]
    slot_count = own_tiles.shape[0]
    block_size = own_tiles.shape[-1]
    candidates = primal_iter.shape[0]
    active = (lax.iota(jnp.int32, slot_count) < tile_counts[0, 0]).astype(jnp.float32)
    primal_group = collect(primal_iter, ROW, 1)
    dual_group = collect(dual_iter, COL, 1)
    column_blocks = primal_group.shape[1] // block_size
    row_blocks = dual_group.shape[1] // block_size
    column_pick = (
        tile_columns[0, 0][:, None] == lax.iota(jnp.int32, column_blocks)[None, :]
    ).astype(jnp.float32)
    column_pick = column_pick * active[:, None]
    row_pick = (tile_rows[0, 0][:, None] == lax.iota(jnp.int32, row_blocks)[None, :]).astype(
        jnp.float32
    )
    row_pick = row_pick * active[:, None]
    primal_pick = jnp.einsum(
        "tc,scb->stb",
        column_pick,
        primal_group.reshape(candidates, column_blocks, block_size),
        precision=HIGHEST_PRECISION,
    )
    dual_pick = jnp.einsum(
        "tr,srb->stb",
        row_pick,
        dual_group.reshape(candidates, row_blocks, block_size),
        precision=HIGHEST_PRECISION,
    )
    tile_product = jnp.einsum("tij,stj->tsi", own_tiles, primal_pick, precision=HIGHEST_PRECISION)
    tile_transposed = jnp.einsum("tij,sti->tsj", own_tiles, dual_pick, precision=HIGHEST_PRECISION)
    row_share = dual_iter.shape[1]
    column_share = primal_iter.shape[1]
    row_start = lax.axis_index(COL) * row_share
    column_start = lax.axis_index(ROW) * column_share
    product_part = jnp.einsum(
        "tr,tsi->sri", row_pick, tile_product, precision=HIGHEST_PRECISION
    ).reshape(candidates, row_blocks * block_size)
    transposed_part = jnp.einsum(
        "tc,tsj->scj", column_pick, tile_transposed, precision=HIGHEST_PRECISION
    ).reshape(candidates, column_blocks * block_size)
    product = sum_at_owner(product_part, COL, 1)
    transposed = sum_at_owner(transposed_part, ROW, 1)
    require_share = lax.dynamic_slice_in_dim(requirement, row_start, row_share)
    kind_share = lax.dynamic_slice_in_dim(constraint_kind, row_start, row_share)
    primal_residual, primal_square, require_square, require_dot = primal_side(
        product, require_share, kind_share, dual_iter
    )
    objective_share = lax.dynamic_slice_in_dim(objective, column_start, column_share)
    lower_share = lax.dynamic_slice_in_dim(lower_bound, column_start, column_share)
    upper_share = lax.dynamic_slice_in_dim(upper_bound, column_start, column_share)
    variable_share = lax.dynamic_slice_in_dim(variable_kind, column_start, column_share)
    dual_residual, dual_square, objective_square, objective_dot, bound_sum = dual_side(
        transposed, objective_share, lower_share, upper_share, variable_share, primal_iter
    )
    statistics = (
        primal_square,
        require_square,
        require_dot,
        dual_square,
        objective_square,
        objective_dot,
        bound_sum,
    )
    statistics = (
        one_axis_at_a_time(statistics[0], ROW_COL),
        one_axis_at_a_time(statistics[1], ROW_COL),
        one_axis_at_a_time(statistics[2], ROW_COL),
        one_axis_at_a_time(statistics[3], ROW_COL),
        one_axis_at_a_time(statistics[4], ROW_COL),
        one_axis_at_a_time(statistics[5], ROW_COL),
        one_axis_at_a_time(statistics[6], ROW_COL),
    )
    (
        primal_square,
        require_square,
        require_dot,
        dual_square,
        objective_square,
        objective_dot,
        bound_sum,
    ) = statistics
    metrics = finish(
        primal_square,
        require_square,
        require_dot,
        dual_square,
        objective_square,
        objective_dot,
        bound_sum,
    )
    return (primal_residual, dual_residual, metrics)


def solution(mesh):
    torus = Mesh(mesh.devices.reshape(4, 2, 2, 4, 2), ("row_0", "row_1", "col_0", "col_1", "col_2"))
    return jax.shard_map(
        on_device,
        mesh=torus,
        in_specs=(
            P(ROW, COL, None, None, None),
            P(ROW, COL, None),
            P(ROW, COL, None),
            P(ROW, COL),
            P(None, COL_ROW),
            P(None, ROW_COL),
            P(ROW),
            P(ROW),
            P(COL),
            P(COL),
            P(COL),
            P(COL),
        ),
        out_specs=(P(None, ROW_COL), P(None, COL_ROW), P()),
        check_vma=False,
    )
```

profile of v0, /device:TPU:1, one launch (start us, length us, event | category | flops | bytes accessed | tf_op | source)
XLA Modules:
  0.0 119.1 jit_solution(9777826574996980370)
XLA Ops:
  0.6 0.0 copy-start.2
  0.6 1.5 %broadcast_in_dim.44 = f32[8,2,4096]{2,1,0:T(2,128)} broadcast(f32[2,4096]{1,0:T(2,128)} %param.16), dimensions={1,2} | broadcast | bytes 294912 | tf_op jit(solution)/shard_map/broadcast_in_dim | solution.py:15
  2.2 8.5 %all-to-all-start = ((f32[8,2,4096]{2,1,0:T(2,128)}), f32[8,2,4096]{2,1,0:T(2,128)S(1)}, u32[]{:S(2)}, u32[]{:S(2)}) async-start(f32[8,2,4096]{2,1,0:T(2,128)} %broadcast_in_dim.44), calls=%async_computation | async-start | bytes 524288 | tf_op jit(solution)/shard_map/all_to_all | solution.py:16
  11.3 0.7 compare_or_fusion.1
  12.0 1.4 %multiply_reduce_fusion.4 = (f32[]{:T(128)}, f32[4096]{0:T(1024)S(1)}, f32[]{:T(128)}, f32[4096]{0:T(1024)S(1)}) fusion(f32[32768]{0:T(1024)} %param.20, s32[]{:T(128)} %select_n.23, f32[65536]{0:T(1024)} %param.18, s32[]{:T(128)S(6)} %select_n.21), kind=kLoop, calls=%fused_computation.21 | loop fusion | flops 16382 | bytes 65552 | tf_op jit(solution)/shard_map/reduce_sum | solution.py:75
  13.5 0.7 compare_or_fusion
  14.2 4.1 %all-to-all-done = f32[8,2,4096]{2,1,0:T(2,128)S(1)} async-done(((f32[8,2,4096]{2,1,0:T(2,128)}), f32[8,2,4096]{2,1,0:T(2,128)S(1)}, u32[]{:S(2)}, u32[]{:S(2)}) %all-to-all-start) | async-done | bytes 262176 | tf_op jit(solution)/shard_map/all_to_all | solution.py:16
  18.3 1.8 %broadcast_in_dim.45 = f32[16,2,4096]{2,1,0:T(2,128)} broadcast(f32[2,4096]{1,0:T(2,128)} %param.17), dimensions={1,2} | broadcast | bytes 557056 | tf_op jit(solution)/shard_map/broadcast_in_dim | solution.py:15
  20.1 6.5 %all-to-all-start.2 = ((f32[16,2,4096]{2,1,0:T(2,128)}), f32[16,2,4096]{2,1,0:T(2,128)S(1)}, u32[]{:S(2)}, u32[]{:S(2)}) async-start(f32[16,2,4096]{2,1,0:T(2,128)} %broadcast_in_dim.45), calls=%async_computation.2 | async-start | bytes 1048576 | tf_op jit(solution)/shard_map/all_to_all | solution.py:16
  26.6 0.2 copy.18
  26.7 0.1 reshape_reshape.12
  26.8 0.9 convolution_bitcast_fusion.2
  27.8 0.0 copy-start.3
  27.8 17.2 %fusion.2 = f32[16,2,512]{2,1,0:T(2,128)S(1)} fusion(f32[1,1,16,512,512]{4,3,2,1,0:T(8,128)} %param.12, f32[2,16,512]{2,1,0:T(8,128)S(1)} %convolution_bitcast_fusion.2), kind=kOutput, calls=%fused_computation.2 | convolution fusion | flops 100663296 | bytes 16908288 | tf_op jit(solution)/shard_map/tij,stj->tsi/dot_general | solution.py:142
  45.0 0.0 copy-start.1
  45.0 0.0 copy-start
  45.0 0.0 dynamic-slice-start
  45.0 0.0 dynamic-slice-start.1
  45.0 0.0 copy-done.2
  45.0 1.0 convolution_bitcast_fusion
  46.0 0.2 copy.21
  46.3 0.1 reshape_reshape.13
  46.4 1.2 %copy.22 = f32[16,2,4096]{2,1,0:T(2,128)} copy(f32[16,2,4096]{2,0,1:T(8,128)S(1)} %bitcast.42) | data formatting | bytes 1048576 | tf_op jit(solution)/shard_map/transpose | solution.py:33
  47.6 0.0 all-to-all-done.2
  47.6 5.7 %all-to-all-start.1 = ((f32[16,2,4096]{2,1,0:T(2,128)}), f32[16,2,4096]{2,1,0:T(2,128)S(1)}, u32[]{:S(2)}, u32[]{:S(2)}) async-start(f32[16,2,4096]{2,1,0:T(2,128)} %copy.22), calls=%async_computation.1 | async-start | bytes 1048576 | tf_op jit(solution)/shard_map/all_to_all | solution.py:38
  53.3 0.3 copy.23
  53.6 0.1 reshape_reshape.14
  53.7 0.4 convolution_bitcast_fusion.3
  54.1 11.5 %fusion = f32[16,2,512]{2,1,0:T(2,128)S(1)} fusion(f32[1,1,16,512,512]{4,3,2,1,0:T(8,128)} %param.12, f32[2,16,512]{2,1,0:T(8,128)S(1)} %convolution_bitcast_fusion.3), kind=kOutput, calls=%fused_computation | convolution fusion | flops 100663296 | bytes 16908288 | tf_op jit(solution)/shard_map/tij,sti->tsj/dot_general | solution.py:143
  65.6 0.0 copy-done.3
  65.6 0.5 convolution_bitcast_fusion.1
  66.1 0.1 reshape_reshape.15
  66.2 0.9 copy.37
  67.1 0.0 all-to-all-done.1
  67.1 3.4 %all-to-all-start.3 = ((f32[8,2,4096]{2,1,0:T(2,128)}), f32[8,2,4096]{2,1,0:T(2,128)S(1)}, u32[]{:S(2)}, u32[]{:S(2)}) async-start(f32[8,2,4096]{2,1,0:T(2,128)} %bitcast.39), calls=%async_computation.3 | async-start | bytes 524288 | tf_op jit(solution)/shard_map/all_to_all | solution.py:38
  70.5 0.7 dynamic-slice_compare_fusion
  71.2 0.2 reduce_sum.81
  71.4 0.0 copy-done.1
  71.4 0.8 multiply_reduce_fusion.3
  72.2 7.0 %all-to-all-done.3 = f32[8,2,4096]{2,1,0:T(2,128)S(1)} async-done(((f32[8,2,4096]{2,1,0:T(2,128)}), f32[8,2,4096]{2,1,0:T(2,128)S(1)}, u32[]{:S(2)}, u32[]{:S(2)}) %all-to-all-start.3) | async-done | bytes 262176 | tf_op jit(solution)/shard_map/all_to_all | solution.py:38
  79.2 0.1 reduce_sum.82
  79.3 0.9 multiply_reduce_fusion.1
  80.2 7.3 %all-reduce.1 = (f32[2]{0:T(128)S(1)}, f32[2]{0:T(128)S(1)}, f32[2]{0:T(128)S(1)}, f32[]{:T(128)}, f32[2]{0:T(128)S(1)}, /*index=5*/f32[]{:T(128)}) all-reduce(f32[2]{0:T(128)S(1)} %add.119, f32[2]{0:T(128)S(1)} %get-tuple-element.12, ...), channel_id=1, replica_groups=mesh['row_0'=4,'row_1'=2,'col_0'=2,'col_1'=4,'col_2'=2] {'row_0'}, use_global_device_ids=true, to_apply=%region_33.34 | all-reduce | flops 10 | bytes 80 | tf_op jit(solution)/shard_map/psum | solution.py:44
  87.5 5.9 %all-reduce.4 = (f32[2]{0:T(128)S(1)}, f32[2]{0:T(128)S(1)}, f32[2]{0:T(128)S(1)}, f32[]{:T(128)}, f32[2]{0:T(128)S(1)}, /*index=5*/f32[]{:T(128)}) all-reduce(f32[2]{0:T(128)S(1)} %get-tuple-element.20, f32[2]{0:T(128)S(1)} %get-tuple-element.21, ...), channel_id=1, replica_groups=mesh['row_0'=4,'row_1'=2,'col_0'=2,'col_1'=4,'col_2'=2] {'row_1'}, use_global_device_ids=true, to_apply=%region_34.35 | all-reduce | flops 10 | bytes 80 | tf_op jit(solution)/shard_map/psum | solution.py:44
  93.4 4.5 %all-reduce.3 = (f32[2]{0:T(128)S(1)}, f32[2]{0:T(128)S(1)}, f32[2]{0:T(128)S(1)}, f32[]{:T(128)}, f32[2]{0:T(128)S(1)}, /*index=5*/f32[]{:T(128)}) all-reduce(f32[2]{0:T(128)S(1)} %get-tuple-element.38, f32[2]{0:T(128)S(1)} %get-tuple-element.39, ...), channel_id=1, replica_groups=mesh['row_0'=4,'row_1'=2,'col_0'=2,'col_1'=4,'col_2'=2] {'col_0'}, use_global_device_ids=true, to_apply=%region_35.36 | all-reduce | flops 10 | bytes 80 | tf_op jit(solution)/shard_map/psum | solution.py:44
  97.9 8.7 %all-reduce = (f32[2]{0:T(128)S(1)}, f32[2]{0:T(128)S(1)}, f32[2]{0:T(128)S(1)}, f32[]{:T(128)}, f32[2]{0:T(128)S(1)}, /*index=5*/f32[]{:T(128)}) all-reduce(f32[2]{0:T(128)S(1)} %get-tuple-element.32, f32[2]{0:T(128)S(1)} %get-tuple-element.33, ...), channel_id=1, replica_groups=mesh['row_0'=4,'row_1'=2,'col_0'=2,'col_1'=4,'col_2'=2] {'col_1'}, use_global_device_ids=true, to_apply=%region_36.37 | all-reduce | flops 10 | bytes 80 | tf_op jit(solution)/shard_map/psum | solution.py:44
  106.6 10.4 %all-reduce.2 = (f32[2]{0:T(128)S(1)}, f32[2]{0:T(128)S(1)}, f32[2]{0:T(128)S(1)}, f32[]{:T(128)}, f32[2]{0:T(128)S(1)}, /*index=5*/f32[]{:T(128)}) all-reduce(f32[2]{0:T(128)S(1)} %get-tuple-element.14, f32[2]{0:T(128)S(1)} %get-tuple-element.15, ...), channel_id=1, replica_groups=mesh['row_0'=4,'row_1'=2,'col_0'=2,'col_1'=4,'col_2'=2] {'col_2'}, use_global_device_ids=true, to_apply=%region_37.38 | all-reduce | flops 10 | bytes 80 | tf_op jit(solution)/shard_map/psum | solution.py:44
  118.5 0.6 copy.27
  (9 shorter events, 0.1 us)
Async XLA Ops:
  0.6 44.4 %copy-start.2 = (s32[1,1,16]{2,1,0:T(1,128)S(1)}, s32[1,1,16]{2,1,0:T(1,128)}, u32[]{:S(2)}) copy-start(s32[1,1,16]{2,1,0:T(1,128)} %param.13) | copy-start | bytes 196
  2.2 16.1 %all-to-all-start = ((f32[8,2,4096]{2,1,0:T(2,128)}), f32[8,2,4096]{2,1,0:T(2,128)S(1)}, u32[]{:S(2)}, u32[]{:S(2)}) async-start(f32[8,2,4096]{2,1,0:T(2,128)} %broadcast_in_dim.44), calls=%async_computation | async-start | bytes 524288 | tf_op jit(solution)/shard_map/all_to_all | solution.py:16
  20.1 27.5 %all-to-all-start.2 = ((f32[16,2,4096]{2,1,0:T(2,128)}), f32[16,2,4096]{2,1,0:T(2,128)S(1)}, u32[]{:S(2)}, u32[]{:S(2)}) async-start(f32[16,2,4096]{2,1,0:T(2,128)} %broadcast_in_dim.45), calls=%async_computation.2 | async-start | bytes 1048576 | tf_op jit(solution)/shard_map/all_to_all | solution.py:16
  27.8 37.8 %copy-start.3 = (s32[1,1,16]{2,1,0:T(1,128)S(1)}, s32[1,1,16]{2,1,0:T(1,128)}, u32[]{:S(2)}) copy-start(s32[1,1,16]{2,1,0:T(1,128)} %param.14) | copy-start | bytes 196
  45.0 26.4 %copy-start.1 = (f32[2,4096]{1,0:T(2,128)S(1)}, f32[2,4096]{1,0:T(2,128)}, u32[]{:S(2)}) copy-start(f32[2,4096]{1,0:T(2,128)} %param.17) | copy-start | bytes 98308
  45.0 34.3 %copy-start = (f32[2,4096]{1,0:T(2,128)S(1)}, f32[2,4096]{1,0:T(2,128)}, u32[]{:S(2)}) copy-start(f32[2,4096]{1,0:T(2,128)} %param.16) | copy-start | bytes 98308
  45.0 34.3 %dynamic-slice-start = ((f32[32768]{0:T(1024)}, s32[]{:T(128)}), f32[4096]{0:T(1024)S(1)}, s32[]{:S(2)}) async-start(f32[32768]{0:T(1024)} %param.21, s32[]{:T(128)} %select_n.23), calls=%async_computation.4 | async-start | bytes 33280 | tf_op jit(solution)/shard_map/dynamic_slice | solution.py:162
  45.0 34.3 %dynamic-slice-start.1 = ((f32[32768]{0:T(1024)}, s32[]{:T(128)}), f32[4096]{0:T(1024)S(1)}, s32[]{:S(2)}) async-start(f32[32768]{0:T(1024)} %param.22, s32[]{:T(128)} %select_n.23), calls=%async_computation.5 | async-start | bytes 33280 | tf_op jit(solution)/shard_map/dynamic_slice | solution.py:163
  47.6 19.5 %all-to-all-start.1 = ((f32[16,2,4096]{2,1,0:T(2,128)}), f32[16,2,4096]{2,1,0:T(2,128)S(1)}, u32[]{:S(2)}, u32[]{:S(2)}) async-start(f32[16,2,4096]{2,1,0:T(2,128)} %copy.22), calls=%async_computation.1 | async-start | bytes 1048576 | tf_op jit(solution)/shard_map/all_to_all | solution.py:38
  67.1 12.1 %all-to-all-start.3 = ((f32[8,2,4096]{2,1,0:T(2,128)}), f32[8,2,4096]{2,1,0:T(2,128)S(1)}, u32[]{:S(2)}, u32[]{:S(2)}) async-start(f32[8,2,4096]{2,1,0:T(2,128)} %bitcast.39), calls=%async_computation.3 | async-start | bytes 524288 | tf_op jit(solution)/shard_map/all_to_all | solution.py:38
where the time goes:
time: 120 us; the launch traced here: 119 us
  blocking collectives  36.8 us (31%)
  matrix products  31.5 us (26%)
  starting transfers between devices  24.1 us (20%)
  waiting for transfers between devices  11.1 us (9%)
  local copies, waits for them, and re-layouts  7.04 us (6%)
  other arithmetic  5.56 us (5%)
  between operations  2.92 us (2%)
    psum x5, blocking collectives, one_axis_at_a_time(): shard = lax.psum(shard, axis)  36.8 us
    dot_general x1, matrix products, on_device(): jnp.einsum('tij,stj->tsi', own_tiles, primal_pick, precision=HIGHEST_PREC...  17.2 us
    all_to_all x2, starting transfers between devices, from_everyone(): return lax.all_to_all(copies, axis, split_axis=0, concat_axis=0, tiled=True)  15 us
    dot_general x1, matrix products, on_device(): jnp.einsum('tij,sti->tsj', own_tiles, dual_pick, precision=HIGHEST_PRECIS...  11.5 us
    all_to_all x2, starting transfers between devices, sum_at_owner(): lax.all_to_all(cut_along(shard, dim, count), axis, 0, 0, tiled=True)  9.13 us
    all_to_all x2, waiting for transfers between devices, sum_at_owner(): lax.all_to_all(cut_along(shard, dim, count), axis, 0, 0, tiled=True)  7 us
    all_to_all x2, waiting for transfers between devices, from_everyone(): return lax.all_to_all(copies, axis, split_axis=0, concat_axis=0, tiled=True)  4.11 us
    broadcast_in_dim x2, local copies, waits for them, and re-layouts, from_everyone(): copies = jnp.broadcast_to(shard, (lax.axis_size(axis), *shard.shape))  3.29 us
  transfers between devices with their start and end apart: 4, of which 2 were waited for; matrix products, arithmetic and copies ran while one was open for 33% of the time, Pallas kernels for 0%

commit v1 on v0

--- a/solution.py
+++ b/solution.py
@@ -41,7 +41,7 @@
 
 def one_axis_at_a_time(shard, axes):
     for axis in axes:
-        shard = lax.psum(shard, axis)
+        shard = jnp.sum(lax.all_gather(shard, axis), axis=0)
     return shard
 
 

time: 120 us -> 151 us (1.26)
  local copies, waits for them, and re-layouts: 7.04 us -> 31.6 us
  other arithmetic: 5.56 us -> 13.4 us
  blocking collectives: 36.8 us -> 32.8 us
  between operations: 2.92 us -> 6.17 us
    psum x5 -> x0, blocking collectives: 36.8 us -> none  [one_axis_at_a_time(): shard = lax.psum(shard, axis)]
    unnamed x0 -> x5, blocking collectives: none -> 32.8 us
    unnamed x9 -> x94, local copies, waits for them, and re-layouts: 0.67 us -> 23.2 us
    reduce_sum x1 -> x37, other arithmetic: 0.86 us -> 8.84 us  [the longest x35 6.65 us: one_axis_at_a_time(): shard = jnp.sum(lax.all_gather(shard, axis), axis=0)]
    all_gather x0 -> x25, local copies, waits for them, and re-layouts: none -> 2.04 us  [one_axis_at_a_time(): shard = jnp.sum(lax.all_gather(shard, axis), axis=0)]
  transfers between devices with their start and end apart: 4 -> 4, of which waited for: 2 -> 3; matrix products, arithmetic and copies ran while one was open for 33% -> 21% of each run, Pallas kernels for 0% -> 0%
where the time goes in v1:
time: 151 us; the launch traced here: 150 us
  blocking collectives  32.8 us (22%)
  local copies, waits for them, and re-layouts  31.6 us (21%)
  matrix products  31.5 us (21%)
  starting transfers between devices  24.9 us (16%)
  other arithmetic  13.4 us (9%)
  waiting for transfers between devices  9.74 us (6%)
  between operations  6.17 us (4%)
    unnamed x5, blocking collectives  32.8 us
    unnamed x94, local copies, waits for them, and re-layouts  23.2 us
    dot_general x1, matrix products, on_device(): jnp.einsum('tij,stj->tsi', own_tiles, primal_pick, precision=HIGHEST_PREC...  17.2 us
    all_to_all x2, starting transfers between devices, from_everyone(): return lax.all_to_all(copies, axis, split_axis=0, concat_axis=0, tiled=True)  15 us
    dot_general x1, matrix products, on_device(): jnp.einsum('tij,sti->tsj', own_tiles, dual_pick, precision=HIGHEST_PRECIS...  11.5 us
    all_to_all x2, starting transfers between devices, sum_at_owner(): lax.all_to_all(cut_along(shard, dim, count), axis, 0, 0, tiled=True)  9.89 us
    reduce_sum x35, other arithmetic, one_axis_at_a_time(): shard = jnp.sum(lax.all_gather(shard, axis), axis=0)  6.65 us
    all_to_all x2, waiting for transfers between devices, sum_at_owner(): lax.all_to_all(cut_along(shard, dim, count), axis, 0, 0, tiled=True)  6.15 us
  transfers between devices with their start and end apart: 4, of which 3 were waited for; matrix products, arithmetic and copies ran while one was open for 21% of the time, Pallas kernels for 0%

profile of v1, /device:TPU:1, one launch (start us, length us, event | category | flops | bytes accessed | tf_op | source)
XLA Modules:
  0.0 150.2 jit_solution(17604487044170105821)
XLA Ops:
  0.6 1.5 %broadcast_in_dim.44 = f32[8,2,4096]{2,1,0:T(2,128)} broadcast(f32[2,4096]{1,0:T(2,128)} %param.16), dimensions={1,2} | broadcast | bytes 294912 | tf_op jit(solution)/shard_map/broadcast_in_dim | solution.py:15
  2.2 8.5 %all-to-all-start = ((f32[8,2,4096]{2,1,0:T(2,128)}), f32[8,2,4096]{2,1,0:T(2,128)S(1)}, u32[]{:S(2)}, u32[]{:S(2)}) async-start(f32[8,2,4096]{2,1,0:T(2,128)} %broadcast_in_dim.44), calls=%async_computation | async-start | bytes 524288 | tf_op jit(solution)/shard_map/all_to_all | solution.py:16
  11.3 0.7 compare_or_fusion.1
  12.0 1.3 multiply_reduce_fusion.4
  13.4 1.3 multiply_reduce_fusion.5
  14.7 3.6 %all-to-all-done = f32[8,2,4096]{2,1,0:T(2,128)S(1)} async-done(((f32[8,2,4096]{2,1,0:T(2,128)}), f32[8,2,4096]{2,1,0:T(2,128)S(1)}, u32[]{:S(2)}, u32[]{:S(2)}) %all-to-all-start) | async-done | bytes 262176 | tf_op jit(solution)/shard_map/all_to_all | solution.py:16
  18.3 1.7 %broadcast_in_dim.45 = f32[16,2,4096]{2,1,0:T(2,128)} broadcast(f32[2,4096]{1,0:T(2,128)} %param.17), dimensions={1,2} | broadcast | bytes 557056 | tf_op jit(solution)/shard_map/broadcast_in_dim | solution.py:15
  20.0 6.5 %all-to-all-start.2 = ((f32[16,2,4096]{2,1,0:T(2,128)}), f32[16,2,4096]{2,1,0:T(2,128)S(1)}, u32[]{:S(2)}, u32[]{:S(2)}) async-start(f32[16,2,4096]{2,1,0:T(2,128)} %broadcast_in_dim.45), calls=%async_computation.2 | async-start | bytes 1048576 | tf_op jit(solution)/shard_map/all_to_all | solution.py:16
  26.8 0.9 convolution_bitcast_fusion.2
  27.7 17.2 %fusion.2 = f32[16,2,512]{2,1,0:T(2,128)S(1)} fusion(f32[1,1,16,512,512]{4,3,2,1,0:T(8,128)} %param.12, f32[2,16,512]{2,1,0:T(8,128)S(1)} %convolution_bitcast_fusion.2), kind=kOutput, calls=%fused_computation.2 | convolution fusion | flops 100663296 | bytes 16908288 | tf_op jit(solution)/shard_map/tij,stj->tsi/dot_general | solution.py:142
  45.9 11.5 %fusion = f32[16,2,512]{2,1,0:T(2,128)S(1)} fusion(f32[1,1,16,512,512]{4,3,2,1,0:T(8,128)} %param.12, f32[2,16,512]{2,1,0:T(8,128)S(1)} %convolution_bitcast_fusion.3), kind=kOutput, calls=%fused_computation | convolution fusion | flops 100663296 | bytes 16908288 | tf_op jit(solution)/shard_map/tij,sti->tsj/dot_general | solution.py:143
  57.9 0.9 copy.37
  58.8 3.6 %all-to-all-start.3 = ((f32[8,2,4096]{2,1,0:T(2,128)}), f32[8,2,4096]{2,1,0:T(2,128)S(1)}, u32[]{:S(2)}, u32[]{:S(2)}) async-start(f32[8,2,4096]{2,1,0:T(2,128)} %bitcast.59), calls=%async_computation.3 | async-start | bytes 524288 | tf_op jit(solution)/shard_map/all_to_all | solution.py:38
  62.4 1.0 convolution_bitcast_fusion
  63.8 1.2 copy.22
  65.0 6.0 %all-to-all-done.3 = f32[8,2,4096]{2,1,0:T(2,128)S(1)} async-done(((f32[8,2,4096]{2,1,0:T(2,128)}), f32[8,2,4096]{2,1,0:T(2,128)S(1)}, u32[]{:S(2)}, u32[]{:S(2)}) %all-to-all-start.3) | async-done | bytes 262176 | tf_op jit(solution)/shard_map/all_to_all | solution.py:38
  71.0 6.3 %all-to-all-start.1 = ((f32[16,2,4096]{2,1,0:T(2,128)}), f32[16,2,4096]{2,1,0:T(2,128)S(1)}, u32[]{:S(2)}, u32[]{:S(2)}) async-start(f32[16,2,4096]{2,1,0:T(2,128)} %copy.22), calls=%async_computation.1 | async-start | bytes 1048576 | tf_op jit(solution)/shard_map/all_to_all | solution.py:38
  77.3 0.7 dynamic-slice_compare_fusion
  78.6 0.7 dynamic-slice.1
  81.6 1.3 dynamic-update-slice.5
  82.9 1.3 dynamic-update-slice.15
  84.2 0.7 compare_or_fusion
  85.1 0.9 add_reduce_fusion
  86.9 0.8 multiply_reduce_fusion.3
  88.2 0.7 dynamic-slice.3
  88.8 6.5 %all-reduce.36 = (f32[8]{0:T(128)S(1)}, f32[8]{0:T(128)S(1)}, f32[8]{0:T(128)S(1)}, f32[8]{0:T(128)S(1)}, f32[4]{0:T(128)S(1)}, /*index=5*/f32[8]{0:T(128)S(1)}, f32[4]{0:T(128)S(1)}) all-reduce(f32[8]{0:T(128)S(1)} %dynamic-update-slice.20, ...), channel_id=12, replica_groups=mesh['row_0'=4,'row_1'=2,'col_0'=2,'col_1'=4,'col_2'=2] {'row_0'}, use_global_device_ids=true, to_apply=%add.20 | all-reduce | flops 48 | bytes 384
  96.8 0.6 reduce_sum.417
  98.3 1.4 dynamic-update-slice.16
  99.7 1.3 dynamic-update-slice.6
  101.7 5.3 %all-reduce.39 = (f32[4]{0:T(128)S(1)}, f32[4]{0:T(128)S(1)}, f32[4]{0:T(128)S(1)}, f32[4]{0:T(128)S(1)}, f32[2]{0:T(128)S(1)}, /*index=5*/f32[4]{0:T(128)S(1)}, f32[2]{0:T(128)S(1)}) all-reduce(f32[4]{0:T(128)S(1)} %dynamic-update-slice.21, ...), channel_id=13, replica_groups=mesh['row_0'=4,'row_1'=2,'col_0'=2,'col_1'=4,'col_2'=2] {'row_1'}, use_global_device_ids=true, to_apply=%add.21 | all-reduce | flops 24 | bytes 192
  108.4 0.6 reduce_sum.418
  109.0 0.6 reduce_sum.406
  109.6 1.3 dynamic-update-slice.17
  110.9 1.3 dynamic-update-slice.7
  112.5 0.6 dynamic-slice.4
  113.1 3.8 %all-reduce.38 = (f32[4]{0:T(128)S(1)}, f32[4]{0:T(128)S(1)}, f32[4]{0:T(128)S(1)}, f32[4]{0:T(128)S(1)}, f32[2]{0:T(128)S(1)}, /*index=5*/f32[4]{0:T(128)S(1)}, f32[2]{0:T(128)S(1)}) all-reduce(f32[4]{0:T(128)S(1)} %dynamic-update-slice.22, ...), channel_id=14, replica_groups=mesh['row_0'=4,'row_1'=2,'col_0'=2,'col_1'=4,'col_2'=2] {'col_0'}, use_global_device_ids=true, to_apply=%add.22 | all-reduce | flops 24 | bytes 192
  118.3 0.6 reduce_sum.419
  118.9 0.7 reduce_sum.407
  119.6 1.4 dynamic-update-slice.18
  121.0 1.4 dynamic-update-slice.8
  123.3 8.4 %all-reduce.35 = (f32[8]{0:T(128)S(1)}, f32[8]{0:T(128)S(1)}, f32[8]{0:T(128)S(1)}, f32[8]{0:T(128)S(1)}, f32[4]{0:T(128)S(1)}, /*index=5*/f32[8]{0:T(128)S(1)}, f32[4]{0:T(128)S(1)}) all-reduce(f32[8]{0:T(128)S(1)} %dynamic-update-slice.23, ...), channel_id=15, replica_groups=mesh['row_0'=4,'row_1'=2,'col_0'=2,'col_1'=4,'col_2'=2] {'col_1'}, use_global_device_ids=true, to_apply=%add.23 | all-reduce | flops 48 | bytes 384
  133.2 0.7 reduce_sum.420
  134.7 1.4 dynamic-update-slice.19
  136.2 1.4 dynamic-update-slice.9
  137.5 8.8 %all-reduce.37 = (f32[4]{0:T(128)S(1)}, f32[4]{0:T(128)S(1)}, f32[4]{0:T(128)S(1)}, f32[4]{0:T(128)S(1)}, f32[2]{0:T(128)S(1)}, /*index=5*/f32[4]{0:T(128)S(1)}, f32[2]{0:T(128)S(1)}) all-reduce(f32[4]{0:T(128)S(1)} %dynamic-update-slice.24, ...), channel_id=16, replica_groups=mesh['row_0'=4,'row_1'=2,'col_0'=2,'col_1'=4,'col_2'=2] {'col_2'}, use_global_device_ids=true, to_apply=%add.24 | all-reduce | flops 24 | bytes 192
  146.4 0.6 reduce_sum.409
  147.7 0.6 reduce_sum.421
  149.5 0.6 copy.27
  (153 shorter events, 13.0 us)
Async XLA Ops:
  0.6 44.9 %copy-start.3 = (s32[1,1,16]{2,1,0:T(1,128)S(1)}, s32[1,1,16]{2,1,0:T(1,128)}, u32[]{:S(2)}) copy-start(s32[1,1,16]{2,1,0:T(1,128)} %param.13) | copy-start | bytes 196
  2.2 16.1 %all-to-all-start = ((f32[8,2,4096]{2,1,0:T(2,128)}), f32[8,2,4096]{2,1,0:T(2,128)S(1)}, u32[]{:S(2)}, u32[]{:S(2)}) async-start(f32[8,2,4096]{2,1,0:T(2,128)} %broadcast_in_dim.44), calls=%async_computation | async-start | bytes 524288 | tf_op jit(solution)/shard_map/all_to_all | solution.py:16
  20.0 25.0 %all-to-all-start.2 = ((f32[16,2,4096]{2,1,0:T(2,128)}), f32[16,2,4096]{2,1,0:T(2,128)S(1)}, u32[]{:S(2)}, u32[]{:S(2)}) async-start(f32[16,2,4096]{2,1,0:T(2,128)} %broadcast_in_dim.45), calls=%async_computation.2 | async-start | bytes 1048576 | tf_op jit(solution)/shard_map/all_to_all | solution.py:16
  27.7 29.6 %copy-start.2 = (s32[1,1,16]{2,1,0:T(1,128)S(1)}, s32[1,1,16]{2,1,0:T(1,128)}, u32[]{:S(2)}) copy-start(s32[1,1,16]{2,1,0:T(1,128)} %param.14) | copy-start | bytes 196
  44.9 33.0 %copy-start.8 = (u32[128]{0:T(128)S(1)}, u32[128]{0:T(128)}, u32[]{:S(2)}) copy-start(u32[128]{0:T(128)} %constant.51) | copy-start | bytes 1540
  44.9 33.6 %copy-start.7 = (u32[128]{0:T(128)S(1)}, u32[128]{0:T(128)}, u32[]{:S(2)}) copy-start(u32[128]{0:T(128)} %constant.56) | copy-start | bytes 1540
  45.0 35.5 %copy-start.6 = (u32[128]{0:T(128)S(1)}, u32[128]{0:T(128)}, u32[]{:S(2)}) copy-start(u32[128]{0:T(128)} %constant.61) | copy-start | bytes 1540
  45.0 40.1 %copy-start = (f32[2,4096]{1,0:T(2,128)S(1)}, f32[2,4096]{1,0:T(2,128)}, u32[]{:S(2)}) copy-start(f32[2,4096]{1,0:T(2,128)} %param.16) | copy-start | bytes 98308
  45.0 40.1 %dynamic-slice-start = ((f32[32768]{0:T(1024)}, s32[]{:T(128)}), f32[4096]{0:T(1024)S(1)}, s32[]{:S(2)}) async-start(f32[32768]{0:T(1024)} %param.21, s32[]{:T(128)} %select_n.23), calls=%async_computation.4 | async-start | bytes 33280 | tf_op jit(solution)/shard_map/dynamic_slice | solution.py:162
  45.0 40.0 %dynamic-slice-start.1 = ((f32[32768]{0:T(1024)}, s32[]{:T(128)}), f32[4096]{0:T(1024)S(1)}, s32[]{:S(2)}) async-start(f32[32768]{0:T(1024)} %param.22, s32[]{:T(128)} %select_n.23), calls=%async_computation.5 | async-start | bytes 33280 | tf_op jit(solution)/shard_map/dynamic_slice | solution.py:163
  45.0 41.9 %copy-start.1 = (f32[2,4096]{1,0:T(2,128)S(1)}, f32[2,4096]{1,0:T(2,128)}, u32[]{:S(2)}) copy-start(f32[2,4096]{1,0:T(2,128)} %param.17) | copy-start | bytes 98308
  45.0 43.2 %copy-start.5 = (u32[128]{0:T(128)S(1)}, u32[128]{0:T(128)}, u32[]{:S(2)}) copy-start(u32[128]{0:T(128)} %constant.66) | copy-start | bytes 1540
  45.0 67.5 %copy-start.4 = (u32[128]{0:T(128)S(1)}, u32[128]{0:T(128)}, u32[]{:S(2)}) copy-start(u32[128]{0:T(128)} %constant.71) | copy-start | bytes 1540
  58.8 12.1 %all-to-all-start.3 = ((f32[8,2,4096]{2,1,0:T(2,128)}), f32[8,2,4096]{2,1,0:T(2,128)S(1)}, u32[]{:S(2)}, u32[]{:S(2)}) async-start(f32[8,2,4096]{2,1,0:T(2,128)} %bitcast.59), calls=%async_computation.3 | async-start | bytes 524288 | tf_op jit(solution)/shard_map/all_to_all | solution.py:38
  71.0 15.8 %all-to-all-start.1 = ((f32[16,2,4096]{2,1,0:T(2,128)}), f32[16,2,4096]{2,1,0:T(2,128)S(1)}, u32[]{:S(2)}, u32[]{:S(2)}) async-start(f32[16,2,4096]{2,1,0:T(2,128)} %copy.22), calls=%async_computation.1 | async-start | bytes 1048576 | tf_op jit(solution)/shard_map/all_to_all | solution.py:38
